TPU v7x, 32 devices: a whole 2x2x4 slice. The times are simulated.
32 devices in a mesh: north: 8 (over y, x, core), east: 4 (over z).
Axes of the slice: x: 2, y: 2, z: 4, core: 2. Of those that a mesh axis runs over, the one named last changes fastest.
Arguments:
- right_side: float32 [512, 256, 256], P('north', 'east'), may hold values from -6 to 6
- first_guess: float32 [512, 256, 256], P('north', 'east'), may hold values from -6 to 6
- mass_term: float32 [512, 256, 256], P('north', 'east'), may hold values from 0.1 to 0.9
Outputs:
- corrected: float32 [512, 256, 256], P('north', 'east')
- remaining: float32 [512, 256, 256], P('north', 'east')
All inputs are finite; a program needn't handle non-finite values.
Results may differ from a plain program's by a relative error of at most 0.000032.
Values sent between devices are 32-bit elements; how exact they have to be, the bound alone decides.
A program may use at most 128 MiB of HBM per device.

v0:
```python
import functools

import jax
import jax.numpy as jnp
from jax import lax
from jax.experimental import pallas as pl
from jax.experimental.pallas import tpu as pltpu
from jax.sharding import PartitionSpec as P

RATIO = 2
INNER = 7
AXES = ("north", "east")
MESH = pl.DeviceIdType.MESH


def ring(axis):
    count, me = lax.axis_size(axis), lax.axis_index(axis)
    return lax.rem(me + count - 1, count), lax.rem(me + 1, count)


def place(axis, index):
    return tuple(index if name == axis else lax.axis_index(name) for name in AXES)


class Level:
    def __init__(self, rows, cols, grids, sent, got, send_sem, recv_sem):
        self.rows, self.cols = rows, cols
        self.grids, self.sent, self.got = grids, sent, got
        self.send_sem, self.recv_sem = send_sem, recv_sem

    def copies(self, p):
        grid = self.grids[p]
        north_low, north_high = ring("north")
        east_low, east_high = ring("east")
        moves = (
            (grid.at[1], grid.at[self.rows + 1], place("north", north_low)),
            (grid.at[self.rows], grid.at[0], place("north", north_high)),
            (self.sent.at[p, 0], self.got.at[p, 1], place("east", east_low)),
            (self.sent.at[p, 1], self.got.at[p, 0], place("east", east_high)),
        )
        return [
            pltpu.make_async_remote_copy(
                src_ref=source,
                dst_ref=target,
                send_sem=self.send_sem.at[p, k],
                recv_sem=self.recv_sem.at[p, k],
                device_id=device,
                device_id_type=MESH,
            )
            for k, (source, target, device) in enumerate(moves)
        ]

    def start(self, p):
        for copy in self.copies(p):
            copy.start()

    def wait(self, p):
        for copy in self.copies(p):
            copy.wait()

    def around(self, p, y, x0, x1):
        grid = self.grids[p]
        a0, a1 = max(x0 - 8, 0), min(x1 + 8, self.cols)
        wide = grid[y, a0:a1, :]
        count = a1 - a0
        low = pltpu.roll(wide, 1, 0)[x0 - a0 : x1 - a0]
        high = pltpu.roll(wide, count - 1, 0)[x0 - a0 : x1 - a0]
        where = lax.broadcasted_iota(jnp.int32, (8, wide.shape[1]), 0)
        if x0 == 0:
            first = jnp.where(where == 0, self.got[p, 0, pl.ds(y - 1, 1), :], low[:8])
            low = first if x1 == 8 else jnp.concatenate([first, low[8:]], axis=0)
        if x1 == self.cols:
            last = jnp.where(where == 7, self.got[p, 1, pl.ds(y - 1, 1), :], high[-8:])
            high = last if x1 - x0 == 8 else jnp.concatenate([high[:-8], last], axis=0)
        total = (low + high) + (grid[y - 1, x0:x1, :] + grid[y + 1, x0:x1, :])
        return wide[x0 - a0 : x1 - a0], total

    def inside(self, cell):
        if self.cols > 16:

            def row(y, carry):
                cell(y, 8, self.cols - 8)
                return carry

            lax.fori_loop(2, self.rows, row, 0, unroll=2)

    def rim(self, cell):
        def row(y, carry):
            cell(y, 0, 8)
            cell(y, self.cols - 8, self.cols)
            return carry

        lax.fori_loop(1, self.rows + 1, row, 0, unroll=4)
        if self.cols > 16:
            cell(1, 8, self.cols - 8)
            cell(self.rows, 8, self.cols - 8)

    def put(self, p, y, x0, x1, new):
        self.grids[p][y, x0:x1, :] = new
        if x0 == 0:
            self.sent[p, 0, pl.ds(y - 1, 1), :] = new[:1]
        if x1 == self.cols:
            self.sent[p, 1, pl.ds(y - 1, 1), :] = new[-1:]

    def sweep(self, p, load, scale):
        def cell(y, x0, x1):
            here, total = self.around(p, y, x0, x1)
            new = 0.2 * here + scale[y - 1, x0:x1, :] * (load[y - 1, x0:x1, :] + total)
            self.put(1 - p, y, x0, x1, new)

        self.start(p)
        self.inside(cell)
        self.wait(p)
        self.rim(cell)


def kernel(
    load_hbm, guess_hbm, mass_hbm, fixed_hbm, left_hbm,
    load, mass, scale, fine_a, fine_b, fine_sent, fine_got,
    thick, cload, cscale, coarse_a, coarse_b, coarse_sent, coarse_got, spread,
    fine_send, fine_recv, coarse_send, coarse_recv, local,
):
    rows, cols, cases = load.shape
    half_rows, half_cols = rows // RATIO, cols // RATIO
    parts = cases // 128
    fine = Level(rows, cols, (fine_a, fine_b), fine_sent, fine_got, fine_send, fine_recv)
    coarse = Level(
        half_rows, half_cols, (coarse_a, coarse_b),
        coarse_sent, coarse_got, coarse_send, coarse_recv,
    )
    fetch_guess = pltpu.make_async_copy(guess_hbm, fine_a.at[pl.ds(1, rows)], local.at[0])
    fetch_mass = pltpu.make_async_copy(mass_hbm, mass, local.at[1])
    fetch_load = pltpu.make_async_copy(load_hbm, load, local.at[2])
    fetch_guess.start()
    fetch_mass.start()
    fetch_load.start()

    barrier = pltpu.get_barrier_semaphore()
    for axis in AXES:
        for other in ring(axis):
            pl.semaphore_signal(barrier, inc=1, device_id=place(axis, other), device_id_type=MESH)
    pl.semaphore_wait(barrier, 4)

    fetch_guess.wait()

    def pack(y, carry):
        fine_sent[0, 0, pl.ds(y, 1), :] = fine_a[y + 1, 0:8, :][:1]
        fine_sent[0, 1, pl.ds(y, 1), :] = fine_a[y + 1, cols - 8 : cols, :][-1:]
        return carry

    lax.fori_loop(0, rows, pack, 0, unroll=4)
    fetch_mass.wait()
    fetch_load.wait()

    def first(y, x0, x1):
        here, total = fine.around(0, y, x0, x1)
        weight = 0.8 / (4.0 + mass[y - 1, x0:x1, :])
        scale[y - 1, x0:x1, :] = weight
        fine.put(1, y, x0, x1, 0.2 * here + weight * (load[y - 1, x0:x1, :] + total))

    fine.start(0)
    fine.inside(first)
    fine.wait(0)
    fine.rim(first)
    fine.sweep(1, load, scale)

    def defect(y, x0, x1):
        here, total = fine.around(0, y, x0, x1)
        return load[y - 1, x0:x1, :] + total - (4.0 + mass[y - 1, x0:x1, :]) * here

    fine.start(0)
    fine.wait(0)

    def gather(y, carry):
        sums = (
            defect(2 * y + 1, 0, cols) + defect(2 * y + 2, 0, cols),
            mass[2 * y] + mass[2 * y + 1],
        )
        for k in range(2):
            for h in range(parts):
                thick[k, h] = sums[k][:, h * 128 : (h + 1) * 128]
        pair = [
            jnp.concatenate(
                [
                    thick.at[k, h][pl.ds(0, half_cols, stride=2), :]
                    + thick.at[k, h][pl.ds(1, half_cols, stride=2), :]
                    for h in range(parts)
                ],
                axis=1,
            )
            for k in range(2)
        ]
        new_load = 0.5 * pair[0]
        weight = 0.8 / (4.0 + 0.5 * pair[1])
        cload[y] = new_load
        cscale[y] = weight
        coarse.put(0, y + 1, 0, half_cols, weight * new_load)
        return carry

    lax.fori_loop(0, half_rows, gather, 0)

    for sweep in range(INNER - 1):
        coarse.sweep(sweep % 2, cload, cscale)
    coarse_last = (coarse_a, coarse_b)[(INNER - 1) % 2]

    def correct(y, carry):
        value = coarse_last[y + 1]
        for h in range(parts):
            part = value[:, h * 128 : (h + 1) * 128]
            spread.at[h][pl.ds(0, half_cols, stride=2), :] = part
            spread.at[h][pl.ds(1, half_cols, stride=2), :] = part
        added = jnp.concatenate([spread[h] for h in range(parts)], axis=1)
        for k in range(2):
            at = 2 * y + 1 + k
            fine.put(1, at, 0, cols, fine_a[at] + added)
        return carry

    lax.fori_loop(0, half_rows, correct, 0)
    fine.sweep(1, load, scale)
    fine.sweep(0, load, scale)

    give_fixed = pltpu.make_async_copy(fine_b.at[pl.ds(1, rows)], fixed_hbm, local.at[0])
    fine.start(1)
    give_fixed.start()

    def left(y, x0, x1):
        here, total = fine.around(1, y, x0, x1)
        scale[y - 1, x0:x1, :] = (
            load[y - 1, x0:x1, :] + total - (4.0 + mass[y - 1, x0:x1, :]) * here
        )

    fine.inside(left)
    fine.wait(1)
    fine.rim(left)
    give_left = pltpu.make_async_copy(scale, left_hbm, local.at[1])
    give_left.start()
    give_fixed.wait()
    give_left.wait()


def body(right_side, first_guess, mass_term):
    rows, cols, cases = right_side.shape
    half_rows, half_cols = rows // RATIO, cols // RATIO
    whole = jax.ShapeDtypeStruct(right_side.shape, jnp.float32)
    any_space = pl.BlockSpec(memory_space=pl.ANY)

    def vmem(*shape):
        return pltpu.VMEM(shape, jnp.float32)

    return pl.pallas_call(
        kernel,
        out_shape=(whole, whole),
        in_specs=[any_space] * 3,
        out_specs=(any_space, any_space),
        scratch_shapes=[
            vmem(rows, cols, cases),
            vmem(rows, cols, cases),
            vmem(rows, cols, cases),
            vmem(rows + 2, cols, cases),
            vmem(rows + 2, cols, cases),
            vmem(2, 2, rows, cases),
            vmem(2, 2, rows, cases),
            vmem(2, cases // 128, cols, 128),
            vmem(half_rows, half_cols, cases),
            vmem(half_rows, half_cols, cases),
            vmem(half_rows + 2, half_cols, cases),
            vmem(half_rows + 2, half_cols, cases),
            vmem(2, 2, half_rows, cases),
            vmem(2, 2, half_rows, cases),
            vmem(cases // 128, cols, 128),
            pltpu.SemaphoreType.DMA((2, 4)),
            pltpu.SemaphoreType.DMA((2, 4)),
            pltpu.SemaphoreType.DMA((2, 4)),
            pltpu.SemaphoreType.DMA((2, 4)),
            pltpu.SemaphoreType.DMA((3,)),
        ],
        compiler_params=pltpu.CompilerParams(
            collective_id=0, has_side_effects=True, vmem_limit_bytes=60 * 1024 * 1024
        ),
    )(right_side, first_guess, mass_term)


def solution(mesh):
    spec = P("north", "east", None)
    return jax.shard_map(
        body, mesh=mesh, in_specs=(spec, spec, spec), out_specs=(spec, spec), check_vma=False
    )
```

profile of v0, /device:TPU:4, one launch (start us, length us, event | category | flops | bytes accessed | tf_op | source)
XLA Modules:
  0.0 78.5 jit_solution(11977054299981604097)
XLA Ops:
  0.6 71.0 %shard_map.50 = (f32[64,64,256]{2,1,0:T(8,128)}, f32[64,64,256]{2,1,0:T(8,128)}) custom-call(f32[64,64,256]{2,1,0:T(8,128)} %load_hbm.1, f32[64,64,256]{2,1,0:T(8,128)} %guess_hbm.1, f32[64,64,256]{2,1,0:T(8,128)} %mass_hbm.1), custom_call_target="tpu_custom_call" | custom-call | tf_op jit(solution)/shard_map/pallas_call | solution.py:250
  71.7 0.0 copy-start
  71.7 4.8 %copy.7 = f32[64,64,256]{2,1,0:T(8,128)} copy(f32[64,64,256]{2,1,0:T(8,128)} %get-tuple-element.4) | data formatting | bytes 8388608
  76.5 0.0 copy-done
  76.5 2.0 %copy.8 = f32[64,64,256]{2,1,0:T(8,128)} copy(f32[64,64,256]{2,1,0:T(8,128)S(1)} %copy-done) | data formatting | bytes 8388608
Async XLA Ops:
  71.7 4.9 %copy-start = (f32[64,64,256]{2,1,0:T(8,128)S(1)}, f32[64,64,256]{2,1,0:T(8,128)}, u32[]{:S(2)}) copy-start(f32[64,64,256]{2,1,0:T(8,128)} %get-tuple-element.5) | copy-start | bytes 12582916
where the time goes:
time: 79.6 us; the launch traced here: 78.5 us
  Pallas kernels  71 us (89%)
  local copies, waits for them, and re-layouts  6.87 us (9%)
    pallas_call x1, Pallas kernels, body(): pl.pallas_call(kernel, out_shape=(whole, whole), in_specs=[any_space] * 3...  71 us
    unnamed x4, local copies, waits for them, and re-layouts  6.87 us

commit v1 on v0

v1 whole, which is shorter than its diff:
```python
import functools

import jax
import jax.numpy as jnp
from jax import lax
from jax.experimental import pallas as pl
from jax.experimental.pallas import tpu as pltpu
from jax.sharding import PartitionSpec as P

RATIO = 2
INNER = 7
NEAR = (INNER - 1) // 2
DEPTH = INNER - NEAR
SCALE_AT = 1
AXES = ("north", "east")
MESH = pl.DeviceIdType.MESH


def ring(axis):
    count, me = lax.axis_size(axis), lax.axis_index(axis)
    return lax.rem(me + count - 1, count), lax.rem(me + 1, count)


def place(axis, index):
    return tuple(index if name == axis else lax.axis_index(name) for name in AXES)


class Level:
    def __init__(self, rows, cols, grids, sent, got, send_sem, recv_sem):
        self.rows, self.cols = rows, cols
        self.grids, self.sent, self.got = grids, sent, got
        self.send_sem, self.recv_sem = send_sem, recv_sem

    def copies(self, p):
        grid = self.grids[p]
        north_low, north_high = ring("north")
        east_low, east_high = ring("east")
        moves = (
            (grid.at[1], grid.at[self.rows + 1], place("north", north_low)),
            (grid.at[self.rows], grid.at[0], place("north", north_high)),
            (self.sent.at[p, 0], self.got.at[p, 1], place("east", east_low)),
            (self.sent.at[p, 1], self.got.at[p, 0], place("east", east_high)),
        )
        return [
            pltpu.make_async_remote_copy(
                src_ref=source,
                dst_ref=target,
                send_sem=self.send_sem.at[p, k],
                recv_sem=self.recv_sem.at[p, k],
                device_id=device,
                device_id_type=MESH,
            )
            for k, (source, target, device) in enumerate(moves)
        ]

    def start(self, p):
        for copy in self.copies(p):
            copy.start()

    def wait(self, p):
        for copy in self.copies(p):
            copy.wait()

    def around(self, p, y, x0, x1, outer=True):
        grid = self.grids[p]
        a0, a1 = max(x0 - 8, 0), min(x1 + 8, self.cols)
        wide = grid[y, a0:a1, :]
        count = a1 - a0
        low = pltpu.roll(wide, 1, 0)[x0 - a0 : x1 - a0]
        high = pltpu.roll(wide, count - 1, 0)[x0 - a0 : x1 - a0]
        where = lax.broadcasted_iota(jnp.int32, (8, wide.shape[1]), 0)
        if x0 == 0:
            first = jnp.where(
                where == 0, self.got[p, 0, pl.ds(y - 1, 1), :] if outer else 0.0, low[:8]
            )
            low = first if x1 == 8 else jnp.concatenate([first, low[8:]], axis=0)
        if x1 == self.cols:
            last = jnp.where(
                where == 7, self.got[p, 1, pl.ds(y - 1, 1), :] if outer else 0.0, high[-8:]
            )
            high = last if x1 - x0 == 8 else jnp.concatenate([high[:-8], last], axis=0)
        total = (low + high) + (grid[y - 1, x0:x1, :] + grid[y + 1, x0:x1, :])
        return wide[x0 - a0 : x1 - a0], total

    def inside(self, cell):
        if self.cols > 16:

            def row(y, carry):
                cell(y, 8, self.cols - 8)
                return carry

            lax.fori_loop(2, self.rows, row, 0, unroll=2)

    def rim(self, cell):
        def row(y, carry):
            cell(y, 0, 8)
            cell(y, self.cols - 8, self.cols)
            return carry

        lax.fori_loop(1, self.rows + 1, row, 0, unroll=4)
        if self.cols > 16:
            cell(1, 8, self.cols - 8)
            cell(self.rows, 8, self.cols - 8)

    def put(self, p, y, x0, x1, new):
        self.grids[p][y, x0:x1, :] = new
        if x0 == 0:
            self.sent[p, 0, pl.ds(y - 1, 1), :] = new[:1]
        if x1 == self.cols:
            self.sent[p, 1, pl.ds(y - 1, 1), :] = new[-1:]

    def sweep(self, p, load, scale, begun=False, own=False):
        def cell(y, x0, x1):
            here, total = self.around(p, y, x0, x1)
            new = 0.2 * here + scale[y - 1, x0:x1, :] * (load[y - 1, x0:x1, :] + total)
            self.put(1 - p, y, x0, x1, new)

        if own:

            def row(y, carry):
                cell(y, 0, self.cols)
                return carry

            lax.fori_loop(1, self.rows + 1, row, 0, unroll=2)
            return
        if not begun:
            self.start(p)
        self.inside(cell)
        self.wait(p)
        self.rim(cell)


def offsets(size, depth, pad, side):
    if side < 0:
        return pad, pad + size, depth
    if side > 0:
        return pad + size - depth, pad - depth, depth
    return pad, pad, size


def deep_copies(wide, depth, size, sends, recvs):
    sides = {axis: (ring(axis)[0], lax.axis_index(axis), ring(axis)[1]) for axis in AXES}
    copies = []
    for dy in (-1, 0, 1):
        for dx in (-1, 0, 1):
            if dy == 0 and dx == 0:
                continue
            from_y, to_y, high = offsets(size[0], depth, DEPTH, dy)
            from_x, to_x, across = offsets(size[1], depth, 8, dx)
            copies.append(
                pltpu.make_async_remote_copy(
                    src_ref=wide.at[pl.ds(from_y, high), pl.ds(from_x, across)],
                    dst_ref=wide.at[pl.ds(to_y, high), pl.ds(to_x, across)],
                    send_sem=sends.at[len(copies)],
                    recv_sem=recvs.at[len(copies)],
                    device_id=(sides["north"][dy + 1], sides["east"][dx + 1]),
                    device_id_type=MESH,
                )
            )
    return copies


def kernel(
    load_hbm, guess_hbm, mass_hbm, fixed, left_out,
    load, mass, scale, fine_a, fine_b, fine_sent, fine_got,
    thick, cload, cscale, coarse_a, coarse_b, coarse_c, spread,
    fine_send, fine_recv, coarse_send, coarse_recv, local,
):
    rows, cols, cases = load.shape
    half_rows, half_cols = rows // RATIO, cols // RATIO
    parts = cases // 128
    fine = Level(rows, cols, (fine_a, fine_b), fine_sent, fine_got, fine_send, fine_recv)
    fetch_guess = pltpu.make_async_copy(guess_hbm, fine_a.at[pl.ds(1, rows)], local.at[0])
    fetch_mass = pltpu.make_async_copy(mass_hbm, mass, local.at[1])
    fetch_load = pltpu.make_async_copy(load_hbm, load, local.at[2])
    fetch_guess.start()
    fetch_mass.start()
    fetch_load.start()

    barrier = pltpu.get_barrier_semaphore()
    norths = (ring("north")[0], lax.axis_index("north"), ring("north")[1])
    easts = (ring("east")[0], lax.axis_index("east"), ring("east")[1])
    for dy in range(3):
        for dx in range(3):
            if (dy, dx) != (1, 1):
                pl.semaphore_signal(
                    barrier, inc=1, device_id=(norths[dy], easts[dx]), device_id_type=MESH
                )
    pl.semaphore_wait(barrier, 8)

    fetch_guess.wait()

    def pack(y, carry):
        fine_sent[0, 0, pl.ds(y, 1), :] = fine_a[y + 1, 0:8, :][:1]
        fine_sent[0, 1, pl.ds(y, 1), :] = fine_a[y + 1, cols - 8 : cols, :][-1:]
        return carry

    lax.fori_loop(0, rows, pack, 0, unroll=4)
    fine.start(0)

    def pairs(k, total):
        for h in range(parts):
            thick[k, h] = total[:, h * 128 : (h + 1) * 128]
        return jnp.concatenate(
            [
                thick.at[k, h][pl.ds(0, half_cols, stride=2), :]
                + thick.at[k, h][pl.ds(1, half_cols, stride=2), :]
                for h in range(parts)
            ],
            axis=1,
        )

    fetch_mass.wait()

    def gather_mass(y, carry):
        total = pairs(0, mass[2 * y] + mass[2 * y + 1])
        cscale[y + DEPTH, 8 : 8 + half_cols, :] = 0.8 / (4.0 + 0.5 * total)
        return carry

    lax.fori_loop(0, half_rows, gather_mass, 0, unroll=2)
    size = (half_rows, half_cols)
    send_scale = deep_copies(cscale, NEAR, size, coarse_send.at[0], coarse_recv.at[0])
    send_load = deep_copies(cload, NEAR, size, coarse_send.at[1], coarse_recv.at[1])
    send_value = deep_copies(coarse_c, DEPTH, size, coarse_send.at[2], coarse_recv.at[2])
    if SCALE_AT == 0:
        for copy in send_scale:
            copy.start()
    fetch_load.wait()

    def first(y, x0, x1):
        here, total = fine.around(0, y, x0, x1)
        weight = 0.8 / (4.0 + mass[y - 1, x0:x1, :])
        scale[y - 1, x0:x1, :] = weight
        fine.put(1, y, x0, x1, 0.2 * here + weight * (load[y - 1, x0:x1, :] + total))

    fine.inside(first)
    fine.wait(0)
    fine.rim(first)
    if SCALE_AT == 1:
        fine.start(1)
        for copy in send_scale:
            copy.start()
        fine.sweep(1, load, scale, begun=True)
    else:
        fine.sweep(1, load, scale)

    def defect(y, outer):
        here, total = fine.around(0, y, 0, cols, outer)
        return load[y - 1] + total - (4.0 + mass[y - 1]) * here

    def gather(y, outer):
        total = pairs(y % 2, defect(2 * y + 1, outer) + defect(2 * y + 2, outer))
        cload[y + DEPTH, 8 : 8 + half_cols, :] = 0.5 * total

    def gather_inner(y, carry):
        gather(y, False)
        return carry

    def gather_outer(y, carry):
        where = lax.broadcasted_iota(jnp.int32, (8, cases), 0)
        low = fine_got[0, 0, pl.ds(2 * y, 1), :] + fine_got[0, 0, pl.ds(2 * y + 1, 1), :]
        high = fine_got[0, 1, pl.ds(2 * y, 1), :] + fine_got[0, 1, pl.ds(2 * y + 1, 1), :]
        cload[y + DEPTH, 8:16, :] += jnp.where(where == 0, 0.5 * low, 0.0)
        cload[y + DEPTH, half_cols : half_cols + 8, :] += jnp.where(where == 7, 0.5 * high, 0.0)
        return carry

    fine.start(0)
    if SCALE_AT == 2:
        for copy in send_scale:
            copy.start()
    lax.fori_loop(1, half_rows - 1, gather_inner, 0, unroll=2)
    fine.wait(0)
    lax.fori_loop(1, half_rows - 1, gather_outer, 0, unroll=2)
    gather(0, True)
    gather(half_rows - 1, True)
    for end in (0, rows + 1):
        fine_b[end] = fine_a[end]
    for side in range(2):
        fine_got[1, side] = fine_got[0, side]
    for copy in send_load:
        copy.start()
    for copy in send_scale:
        copy.wait()
    for copy in send_load:
        copy.wait()

    tall, broad = cload.shape[0], cload.shape[1]

    def begin(y, carry):
        coarse_a[y] = cscale[y] * cload[y]
        return carry

    margin = DEPTH - NEAR
    lax.fori_loop(margin, tall - margin, begin, 0, unroll=2)

    def sweeps(chain, margin):
        for step, (old, new) in enumerate(zip(chain, chain[1:]), 1):
            own = new is coarse_c

            def row(y, carry, old=old, new=new, own=own):
                here = old[y]
                total = (pltpu.roll(here, 1, 0) + pltpu.roll(here, broad - 1, 0)) + (
                    old[y - 1] + old[y + 1]
                )
                value = 0.2 * here + cscale[y] * (cload[y] + total)
                if own:
                    new[y, 8 : 8 + half_cols, :] = value[8 : 8 + half_cols]
                else:
                    new[y] = value
                return carry

            lax.fori_loop(margin + step, tall - margin - step, row, 0, unroll=2)

    grids = (coarse_a, coarse_b)
    sweeps([grids[step % 2] for step in range(NEAR)] + [coarse_c], margin)
    for copy in send_value:
        copy.start()
    for copy in send_value:
        copy.wait()
    rest = INNER - 1 - NEAR
    sweeps([coarse_c] + [grids[step % 2] for step in range(rest)], 0)
    last = grids[(rest - 1) % 2]

    def widen(k, y):
        for h in range(parts):
            part = last[y, 8 : 8 + half_cols, h * 128 : (h + 1) * 128]
            spread.at[k, h][pl.ds(0, half_cols, stride=2), :] = part
            spread.at[k, h][pl.ds(1, half_cols, stride=2), :] = part
        return jnp.concatenate([spread[k, h] for h in range(parts)], axis=1)

    def correct(y, carry):
        added = widen(y % 2, y + DEPTH)
        low = last[y + DEPTH, 0:8, :][-1:]
        high = last[y + DEPTH, 8 + half_cols : 16 + half_cols, :][:1]
        for k in range(2):
            at = 2 * y + 1 + k
            fine_b[at] = fine_a[at] + added
            fine_got[1, 0, pl.ds(at - 1, 1), :] += low
            fine_got[1, 1, pl.ds(at - 1, 1), :] += high
        return carry

    lax.fori_loop(0, half_rows, correct, 0, unroll=2)
    fine_b[0] += widen(0, DEPTH - 1)
    fine_b[rows + 1] += widen(1, DEPTH + half_rows)
    fine.sweep(1, load, scale, own=True)
    fine.sweep(0, load, scale)

    def left(y, x0, x1):
        here, total = fine.around(1, y, x0, x1)
        fixed[y - 1, x0:x1, :] = here
        left_out[y - 1, x0:x1, :] = (
            load[y - 1, x0:x1, :] + total - (4.0 + mass[y - 1, x0:x1, :]) * here
        )

    fine.start(1)
    fine.inside(left)
    fine.wait(1)
    fine.rim(left)


def body(right_side, first_guess, mass_term):
    rows, cols, cases = right_side.shape
    half_rows, half_cols = rows // RATIO, cols // RATIO
    whole = jax.ShapeDtypeStruct(right_side.shape, jnp.float32)
    any_space = pl.BlockSpec(memory_space=pl.ANY)

    def vmem(*shape):
        return pltpu.VMEM(shape, jnp.float32)

    fixed, left = pl.pallas_call(
        kernel,
        out_shape=(pltpu.VMEM(right_side.shape, jnp.float32), pltpu.VMEM(right_side.shape, jnp.float32)),
        in_specs=[any_space] * 3,
        out_specs=(pl.BlockSpec(memory_space=pltpu.VMEM),)*2,
        scratch_shapes=[
            vmem(rows, cols, cases),
            vmem(rows, cols, cases),
            vmem(rows, cols, cases),
            vmem(rows + 2, cols, cases),
            vmem(rows + 2, cols, cases),
            vmem(2, 2, rows, cases),
            vmem(2, 2, rows, cases),
            vmem(2, cases // 128, cols, 128),
            vmem(half_rows + 2 * DEPTH, half_cols + 16, cases),
            vmem(half_rows + 2 * DEPTH, half_cols + 16, cases),
            vmem(half_rows + 2 * DEPTH, half_cols + 16, cases),
            vmem(half_rows + 2 * DEPTH, half_cols + 16, cases),
            vmem(half_rows + 2 * DEPTH, half_cols + 16, cases),
            vmem(2, cases // 128, cols, 128),
            pltpu.SemaphoreType.DMA((2, 4)),
            pltpu.SemaphoreType.DMA((2, 4)),
            pltpu.SemaphoreType.DMA((3, 8)),
            pltpu.SemaphoreType.DMA((3, 8)),
            pltpu.SemaphoreType.DMA((3,)),
        ],
        compiler_params=pltpu.CompilerParams(
            collective_id=0, has_side_effects=True, vmem_limit_bytes=48 * 1024 * 1024
        ),
    )(right_side, first_guess, mass_term)
    return fixed, left


def solution(mesh):
    spec = P("north", "east", None)
    return jax.shard_map(
        body, mesh=mesh, in_specs=(spec, spec, spec), out_specs=(spec, spec), check_vma=False
    )
```

time: 79.6 us -> 64.4 us (0.81); the launches traced: 78.5 us -> 64.3 us
  Pallas kernels: 71 us -> 59.6 us
  local copies, waits for them, and re-layouts: 6.87 us -> 4.03 us
    pallas_call x1, Pallas kernels: 71 us -> 59.6 us  [body(): pl.pallas_call(kernel, out_shape=(pltpu.VMEM(right_side.shape, jnp.float3...]
    unnamed x4 -> x2, local copies, waits for them, and re-layouts: 6.87 us -> 4.03 us
where the time goes in v1:
time: 64.4 us; the launch traced here: 64.3 us
  Pallas kernels  59.6 us (93%)
  local copies, waits for them, and re-layouts  4.03 us (6%)
    pallas_call x1, Pallas kernels, body(): pl.pallas_call(kernel, out_shape=(pltpu.VMEM(right_side.shape, jnp.float3...  59.6 us
    unnamed x2, local copies, waits for them, and re-layouts  4.03 us

profile of v1, /device:TPU:4, one launch (start us, length us, event | category | flops | bytes accessed | tf_op | source)
XLA Modules:
  0.0 64.3 jit_solution(15213891025246473957)
XLA Ops:
  0.6 59.6 %shard_map.50 = (f32[64,64,256]{2,1,0:T(8,128)S(1)}, f32[64,64,256]{2,1,0:T(8,128)S(1)}) custom-call(f32[64,64,256]{2,1,0:T(8,128)} %load_hbm.1, f32[64,64,256]{2,1,0:T(8,128)} %guess_hbm.1, f32[64,64,256]{2,1,0:T(8,128)} %mass_hbm.1), custom_call_target="tpu_custom_call" | custom-call | tf_op jit(solution)/shard_map/pallas_call | solution.py:370
  60.3 2.0 %copy.7 = f32[64,64,256]{2,1,0:T(8,128)} copy(f32[64,64,256]{2,1,0:T(8,128)S(1)} %get-tuple-element.2) | data formatting | bytes 8388608
  62.3 2.0 %copy.8 = f32[64,64,256]{2,1,0:T(8,128)} copy(f32[64,64,256]{2,1,0:T(8,128)S(1)} %get-tuple-element.3) | data formatting | bytes 8388608

commit v2 on v1

--- a/solution.py
+++ b/solution.py
@@ -11,7 +11,7 @@
 INNER = 7
 NEAR = (INNER - 1) // 2
 DEPTH = INNER - NEAR
-SCALE_AT = 1
+SCALE_AT = 0
 AXES = ("north", "east")
 MESH = pl.DeviceIdType.MESH
 
@@ -83,37 +83,44 @@
         return wide[x0 - a0 : x1 - a0], total
 
     def inside(self, cell):
-        if self.cols > 16:
-
-            def row(y, carry):
-                cell(y, 8, self.cols - 8)
-                return carry
-
-            lax.fori_loop(2, self.rows, row, 0, unroll=2)
-
-    def rim(self, cell):
         def row(y, carry):
-            cell(y, 0, 8)
-            cell(y, self.cols - 8, self.cols)
+            cell(y, 0, self.cols, False)
             return carry
 
-        lax.fori_loop(1, self.rows + 1, row, 0, unroll=4)
-        if self.cols > 16:
-            cell(1, 8, self.cols - 8)
-            cell(self.rows, 8, self.cols - 8)
-
-    def put(self, p, y, x0, x1, new):
+        lax.fori_loop(2, self.rows, row, 0, unroll=2)
+
+    def rim(self, p, cell, mend):
+        def row(y, carry):
+            low = self.got[p, 0, pl.ds(y - 1, 1), :]
+            high = self.got[p, 1, pl.ds(y - 1, 1), :]
+            where = lax.broadcasted_iota(jnp.int32, (8, low.shape[1]), 0)
+            mend(y, 0, 8, jnp.where(where == 0, low, 0.0))
+            mend(y, self.cols - 8, self.cols, jnp.where(where == 7, high, 0.0))
+            return carry
+
+        lax.fori_loop(2, self.rows, row, 0, unroll=4)
+        cell(1, 0, self.cols)
+        cell(self.rows, 0, self.cols)
+
+    def put(self, p, y, x0, x1, new, outer=True):
         self.grids[p][y, x0:x1, :] = new
-        if x0 == 0:
+        if outer and x0 == 0:
             self.sent[p, 0, pl.ds(y - 1, 1), :] = new[:1]
-        if x1 == self.cols:
+        if outer and x1 == self.cols:
             self.sent[p, 1, pl.ds(y - 1, 1), :] = new[-1:]
 
+    def mend(self, p, scale):
+        def add(y, x0, x1, more):
+            old = self.grids[1 - p][y, x0:x1, :]
+            self.put(1 - p, y, x0, x1, old + scale[y - 1, x0:x1, :] * more)
+
+        return add
+
     def sweep(self, p, load, scale, begun=False, own=False):
-        def cell(y, x0, x1):
-            here, total = self.around(p, y, x0, x1)
+        def cell(y, x0, x1, outer=True):
+            here, total = self.around(p, y, x0, x1, outer)
             new = 0.2 * here + scale[y - 1, x0:x1, :] * (load[y - 1, x0:x1, :] + total)
-            self.put(1 - p, y, x0, x1, new)
+            self.put(1 - p, y, x0, x1, new, outer)
 
         if own:
 
@@ -127,7 +134,7 @@
             self.start(p)
         self.inside(cell)
         self.wait(p)
-        self.rim(cell)
+        self.rim(p, cell, self.mend(p, scale))
 
 
 def offsets(size, depth, pad, side):
@@ -174,8 +181,6 @@
     fetch_mass = pltpu.make_async_copy(mass_hbm, mass, local.at[1])
     fetch_load = pltpu.make_async_copy(load_hbm, load, local.at[2])
     fetch_guess.start()
-    fetch_mass.start()
-    fetch_load.start()
 
     barrier = pltpu.get_barrier_semaphore()
     norths = (ring("north")[0], lax.axis_index("north"), ring("north")[1])
@@ -189,6 +194,8 @@
     pl.semaphore_wait(barrier, 8)
 
     fetch_guess.wait()
+    fetch_mass.start()
+    fetch_load.start()
 
     def pack(y, carry):
         fine_sent[0, 0, pl.ds(y, 1), :] = fine_a[y + 1, 0:8, :][:1]
@@ -227,15 +234,15 @@
             copy.start()
     fetch_load.wait()
 
-    def first(y, x0, x1):
-        here, total = fine.around(0, y, x0, x1)
+    def first(y, x0, x1, outer=True):
+        here, total = fine.around(0, y, x0, x1, outer)
         weight = 0.8 / (4.0 + mass[y - 1, x0:x1, :])
         scale[y - 1, x0:x1, :] = weight
-        fine.put(1, y, x0, x1, 0.2 * here + weight * (load[y - 1, x0:x1, :] + total))
+        fine.put(1, y, x0, x1, 0.2 * here + weight * (load[y - 1, x0:x1, :] + total), outer)
 
     fine.inside(first)
     fine.wait(0)
-    fine.rim(first)
+    fine.rim(0, first, fine.mend(0, scale))
     if SCALE_AT == 1:
         fine.start(1)
         for copy in send_scale:
@@ -309,7 +316,7 @@
                     new[y] = value
                 return carry
 
-            lax.fori_loop(margin + step, tall - margin - step, row, 0, unroll=2)
+            lax.fori_loop(margin + step, tall - margin - step, row, 0, unroll=4)
 
     grids = (coarse_a, coarse_b)
     sweeps([grids[step % 2] for step in range(NEAR)] + [coarse_c], margin)
@@ -345,8 +352,8 @@
     fine.sweep(1, load, scale, own=True)
     fine.sweep(0, load, scale)
 
-    def left(y, x0, x1):
-        here, total = fine.around(1, y, x0, x1)
+    def left(y, x0, x1, outer=True):
+        here, total = fine.around(1, y, x0, x1, outer)
         fixed[y - 1, x0:x1, :] = here
         left_out[y - 1, x0:x1, :] = (
             load[y - 1, x0:x1, :] + total - (4.0 + mass[y - 1, x0:x1, :]) * here
@@ -355,7 +362,11 @@
     fine.start(1)
     fine.inside(left)
     fine.wait(1)
-    fine.rim(left)
+
+    def mend_left(y, x0, x1, more):
+        left_out[y - 1, x0:x1, :] += more
+
+    fine.rim(1, left, mend_left)
 
 
 def body(right_side, first_guess, mass_term):

time: 64.4 us -> 63 us (0.978)
  Pallas kernels: 59.6 us -> 58.1 us
    pallas_call x1, Pallas kernels: 59.6 us -> 58.1 us  [body(): pl.pallas_call(kernel, out_shape=(pltpu.VMEM(right_side.shape, jnp.float3...]
where the time goes in v2:
time: 63 us; the launch traced here: 62.8 us
  Pallas kernels  58.1 us (92%)
  local copies, waits for them, and re-layouts  4.03 us (6%)
  between operations  0.64 us (1%)
    pallas_call x1, Pallas kernels, body(): pl.pallas_call(kernel, out_shape=(pltpu.VMEM(right_side.shape, jnp.float3...  58.1 us
    unnamed x2, local copies, waits for them, and re-layouts  4.03 us

profile of v2, /device:TPU:4, one launch (start us, length us, event | category | flops | bytes accessed | tf_op | source)
XLA Modules:
  0.0 62.8 jit_solution(10351808640394270312)
XLA Ops:
  0.6 58.1 %shard_map.50 = (f32[64,64,256]{2,1,0:T(8,128)S(1)}, f32[64,64,256]{2,1,0:T(8,128)S(1)}) custom-call(f32[64,64,256]{2,1,0:T(8,128)} %load_hbm.1, f32[64,64,256]{2,1,0:T(8,128)} %guess_hbm.1, f32[64,64,256]{2,1,0:T(8,128)} %mass_hbm.1), custom_call_target="tpu_custom_call" | custom-call | tf_op jit(solution)/shard_map/pallas_call | solution.py:381
  58.8 2.0 %copy.7 = f32[64,64,256]{2,1,0:T(8,128)} copy(f32[64,64,256]{2,1,0:T(8,128)S(1)} %get-tuple-element.2) | data formatting | bytes 8388608
  60.8 2.0 %copy.8 = f32[64,64,256]{2,1,0:T(8,128)} copy(f32[64,64,256]{2,1,0:T(8,128)S(1)} %get-tuple-element.3) | data formatting | bytes 8388608
